TPU v7x, 32 devices: a whole 2x2x4 slice. The times are simulated.
32 devices in a mesh: gx: 4 (over z), gy: 2 (over x), gz: 4 (over y, core).
Axes of the slice: x: 2, y: 2, z: 4, core: 2. Of those that a mesh axis runs over, the one named last changes fastest.
Arguments:
- attn_out: bfloat16 [16384, 8192], P('gx', ('gy', 'gz')), may hold values from -6 to 6
- out_grad: bfloat16 [16384, 8192], P('gx', ('gz', 'gy')), may hold values from -0.046875 to 0.046875
- valid_counts: int32 [16], P('gx'), may hold values from 128 to 1024
Outputs:
- weight_grad: float32 [8192, 8192], P(('gy', 'gx'), 'gz')
Inputs may be any that keep to these rules, and one draw needn't show every extreme that they name: `valid_counts`: valid tokens of a packed row come first, padding after.
All inputs are finite; a program needn't handle non-finite values.
Results may differ from a plain program's by a relative error of at most 0.0003.
Values may be sent and summed in bfloat16 or wider, within the bound.
No kernel may reach another device: no remote copies, remote signals or barrier semaphores. Data moves between devices by JAX's collectives and lax.ppermute only.
A program may use at most 192 MiB of HBM per device.

v0:
```python
import jax
import jax.numpy as jnp
from jax import lax
from jax.sharding import PartitionSpec as P


def transpose_product(inputs, grads):
    return lax.dot_general(
        inputs, grads, (((0,), (0,)), ((), ())), preferred_element_type=jnp.float32
    )


def shards(attn_out, out_grad, valid_counts):
    rows_here = valid_counts.shape[0]
    slot_count = attn_out.shape[0] // rows_here
    positions = lax.broadcasted_iota(jnp.int32, (rows_here, slot_count), 1)
    kept_rows = (positions < valid_counts[:, None]).reshape(-1)
    gathered_inputs = lax.all_gather(attn_out, "gz", axis=1, tiled=True)
    gathered_grads = lax.all_gather(out_grad, "gy", axis=1, tiled=True)
    masked = jnp.where(kept_rows[:, None], gathered_grads, jnp.zeros((), gathered_grads.dtype))
    partial_grad = transpose_product(gathered_inputs, masked)
    return lax.psum_scatter(partial_grad, "gx", scatter_dimension=0, tiled=True)


def solution(mesh):
    in_specs = (P("gx", ("gy", "gz")), P("gx", ("gz", "gy")), P("gx"))
    out_specs = P(("gy", "gx"), "gz")
    return jax.shard_map(shards, mesh=mesh, in_specs=in_specs, out_specs=out_specs, check_vma=False)
```

profile of v0, /device:TPU:0, one launch (start us, length us, event | category | flops | bytes accessed | tf_op | source)
XLA Modules:
  0.0 1061.9 jit_solution(18123328808910169511)
XLA Ops:
  6.5 0.0 copy-start
  6.5 0.0 all-gather.3.cloned.1.call-start
  6.5 0.7 all-gather.3.cloned.1.call-update
  7.3 0.0 all-gather.5.cloned.1.call-start
  7.3 0.7 all-gather.5.cloned.1.call-update
  8.0 0.0 reduce-scatter.2.cloned.1.call-start
  8.1 0.0 copy-done
  8.1 0.1 fusion.3
  8.2 202.3 %all-gather.3.cloned.1.call-done = bf16[4096,2048]{1,0:T(8,128)(2,1)} async-done(((bf16[4096,1024]{1,0:T(8,128)(2,1)}), bf16[4096,2048]{1,0:T(8,128)(2,1)}) %all-gather.3.cloned.1.call-update) | async-done | bytes 16777232 | tf_op jit(solution)/shard_map/all_gather | solution.py:19
  210.5 203.1 %all-gather.5.cloned.1.call-done = bf16[4096,4096]{1,0:T(8,128)(2,1)} async-done(((bf16[4096,1024]{1,0:T(8,128)(2,1)}), bf16[4096,4096]{1,0:T(8,128)(2,1)}) %all-gather.5.cloned.1.call-update) | async-done | bytes 33554448 | tf_op jit(solution)/shard_map/all_gather | solution.py:18
  413.6 80.3 %convolution_bitcast_fusion = f32[4096,2048]{0,1:T(8,128)} fusion(bf16[4096,4096]{1,0:T(8,128)(2,1)} %all-gather.5.cloned.1.call-done, bf16[4096,2048]{1,0:T(8,128)(2,1)} %all-gather.3.cloned.1.call-done, pred[4096]{0:T(1024)(128)(4,1)S(1)} %bitcast.10), kind=kOutput, calls=%fused_computation | convolution fusion | flops 68727865344 | bytes 83890176 | tf_op jit(solution)/shard_map/dot_general | solution.py:8
  493.9 0.0 reduce-scatter.2.cloned.1.call-update
  493.9 552.4 %reduce-scatter.2.cloned.1.call-done = f32[1024,2048]{0,1:T(8,128)} async-done(((f32[4096,2048]{0,1:T(8,128)}), f32[1024,2048]{0,1:T(8,128)}) %reduce-scatter.2.cloned.1.call-update) | async-done | bytes 8388624 | tf_op jit(solution)/shard_map/reduce_scatter | solution.py:22
  1046.3 9.1 copy.4
  (1 shorter events, 0.0 us)
Async XLA Ops:
  6.5 1.5 copy-start
  6.5 203.9 %all-gather.3.cloned.1.call-start = ((), (), s32[]{:S(2)}) async-start(), calls=%async_computation.1 | async-start | bytes 25165824 | tf_op jit(solution)/shard_map/all_gather | solution.py:19
  7.3 406.3 %all-gather.5.cloned.1.call-start = ((), (), s32[]{:S(2)}) async-start(), calls=%async_computation.2 | async-start | bytes 41943040 | tf_op jit(solution)/shard_map/all_gather | solution.py:18
  8.0 1038.2 %reduce-scatter.2.cloned.1.call-start = ((), (), s32[]{:S(2)}) async-start(), calls=%async_computation.3 | async-start | bytes 41943040 | tf_op jit(solution)/shard_map/reduce_scatter | solution.py:22
Sparse Core Ops, SparseCore 0:
  8.9 201.5 all-gather.2
  212.1 201.4 all-gather.4
  494.0 552.2 reduce-scatter.1
where the time goes:
time: 1060 us
  waiting for transfers between devices  959 us (90%)
  matrix products  80.3 us (8%)
  between operations  13.1 us (1%)
    reduce_scatter x1, waiting for transfers between devices, shards(): return lax.psum_scatter(partial_grad, 'gx', scatter_dimension=0, tiled=True)  552 us
    all_gather x1, waiting for transfers between devices, shards(): gathered_inputs = lax.all_gather(attn_out, 'gz', axis=1, tiled=True)  203 us
    all_gather x1, waiting for transfers between devices, shards(): gathered_grads = lax.all_gather(out_grad, 'gy', axis=1, tiled=True)  202 us
    dot_general x1, matrix products, transpose_product(): lax.dot_general(inputs, grads, (((0,), (0,)), ((), ())), preferred_elemen...  80.3 us
  transfers between devices with their start and end apart: 3, of which 3 were waited for; matrix products, arithmetic and copies ran while one was open for 0% of the time, Pallas kernels for 0%

commit v1 on v0

--- a/solution.py
+++ b/solution.py
@@ -15,7 +15,12 @@
     slot_count = attn_out.shape[0] // rows_here
     positions = lax.broadcasted_iota(jnp.int32, (rows_here, slot_count), 1)
     kept_rows = (positions < valid_counts[:, None]).reshape(-1)
-    gathered_inputs = lax.all_gather(attn_out, "gz", axis=1, tiled=True)
+    ring = [attn_out]
+    for hop in range(3):
+        ring.append(lax.ppermute(ring[-1], "gz", [(dev, (dev + 1) % 4) for dev in range(4)]))
+    gathered_inputs = jnp.roll(
+        jnp.concatenate(ring[::-1], axis=1), (lax.axis_index("gz") + 1) * ring[0].shape[1], axis=1
+    )
     gathered_grads = lax.all_gather(out_grad, "gy", axis=1, tiled=True)
     masked = jnp.where(kept_rows[:, None], gathered_grads, jnp.zeros((), gathered_grads.dtype))
     partial_grad = transpose_product(gathered_inputs, masked)

time: 1060 us -> 989 us (0.933)
  waiting for transfers between devices: 959 us -> 833 us
  local copies, waits for them, and re-layouts: 9.14 us -> 60.5 us
    ppermute x0 -> x3, waiting for transfers between devices: none -> 279 us  [shards(): lax.ppermute(ring[-1], 'gz', [(dev, (dev + 1) % 4) for dev in range(4)])]
    all_gather x1 -> x0, waiting for transfers between devices: 203 us -> none  [shards(): gathered_inputs = lax.all_gather(attn_out, 'gz', axis=1, tiled=True)]
    all_gather x1, waiting for transfers between devices: 202 us -> 0.01 us  [shards(): gathered_grads = lax.all_gather(out_grad, 'gy', axis=1, tiled=True)]
    unnamed x3 -> x8, local copies, waits for them, and re-layouts: 0.01 us -> 53 us
  transfers between devices with their start and end apart: 3 -> 5, of which waited for: 3 -> 4; matrix products, arithmetic and copies ran while one was open for 0% -> 6% of each run, Pallas kernels for 0% -> 0%
where the time goes in v1:
time: 989 us
  waiting for transfers between devices  833 us (84%)
  matrix products  80.1 us (8%)
  local copies, waits for them, and re-layouts  60.5 us (6%)
  between operations  13.4 us (1%)
    reduce_scatter x1, waiting for transfers between devices, shards(): return lax.psum_scatter(partial_grad, 'gx', scatter_dimension=0, tiled=True)  554 us
    ppermute x3, waiting for transfers between devices, shards(): lax.ppermute(ring[-1], 'gz', [(dev, (dev + 1) % 4) for dev in range(4)])  279 us
    dot_general x1, matrix products, transpose_product(): lax.dot_general(inputs, grads, (((0,), (0,)), ((), ())), preferred_elemen...  80.1 us
    unnamed x8, local copies, waits for them, and re-layouts  53 us
  transfers between devices with their start and end apart: 5, of which 4 were waited for; matrix products, arithmetic and copies ran while one was open for 6% of the time, Pallas kernels for 0%

profile of v1, /device:TPU:0, one launch (start us, length us, event | category | flops | bytes accessed | tf_op | source)
XLA Modules:
  0.0 988.7 jit_solution(15914844357504711580)
XLA Ops:
  6.5 0.0 all-gather.2.cloned.1.call-start
  6.5 0.5 collective-permute-start
  7.0 93.4 %collective-permute-done = bf16[4096,1024]{1,0:T(8,128)(2,1)} collective-permute-done((bf16[4096,1024]{1,0:T(8,128)(2,1)}, bf16[4096,1024]{1,0:T(8,128)(2,1)}, u32[]{:S(2)}, u32[]{:S(2)}) %collective-permute-start) | collective-permute-done | bytes 8388640 | tf_op jit(solution)/shard_map/ppermute | solution.py:20
  100.4 0.0 collective-permute-start.1
  100.4 0.0 all-gather.2.cloned.1.call-update
  100.4 0.0 reduce-scatter.2.cloned.1.call-start
  100.5 93.1 %collective-permute-done.1 = bf16[4096,1024]{1,0:T(8,128)(2,1)} collective-permute-done((bf16[4096,1024]{1,0:T(8,128)(2,1)}, bf16[4096,1024]{1,0:T(8,128)(2,1)}, u32[]{:S(2)}, u32[]{:S(2)}) %collective-permute-start.1) | collective-permute-done | bytes 8388640 | tf_op jit(solution)/shard_map/ppermute | solution.py:20
  193.6 0.0 collective-permute-start.2
  193.6 0.7 fusion.5
  194.4 92.4 %collective-permute-done.2 = bf16[4096,1024]{1,0:T(8,128)(2,1)} collective-permute-done((bf16[4096,1024]{1,0:T(8,128)(2,1)}, bf16[4096,1024]{1,0:T(8,128)(2,1)}, u32[]{:S(2)}, u32[]{:S(2)}) %collective-permute-start.2) | collective-permute-done | bytes 8388640 | tf_op jit(solution)/shard_map/ppermute | solution.py:20
  286.8 7.5 constant_dynamic-update-slice_fusion.7
  294.3 7.6 constant_dynamic-update-slice_fusion.6
  301.9 7.6 constant_dynamic-update-slice_fusion.5
  309.6 7.6 constant_dynamic-update-slice_fusion.4
  317.1 7.5 constant_dynamic-update-slice_fusion.3
  324.7 7.6 constant_dynamic-update-slice_fusion.2
  332.2 7.5 constant_dynamic-update-slice_fusion.1
  339.7 7.6 constant_dynamic-update-slice_fusion
  347.3 0.0 all-gather.2.cloned.1.call-done
  347.3 80.1 %fusion = f32[4096,2048]{1,0:T(8,128)} fusion(bf16[4096,8192]{1,0:T(8,128)(2,1)} %constant_dynamic-update-slice_fusion, s32[]{:T(128)S(6)} %select_n.18, bf16[4096,2048]{1,0:T(8,128)(2,1)} %all-gather.2.cloned.1.call-done, pred[4096]{0:T(1024)(128)(4,1)S(1)} %bitcast.5), kind=kOutput, calls=%fused_computation | convolution fusion | flops 68727865344 | bytes 83890176 | tf_op jit(solution)/shard_map/dot_general | solution.py:8
  427.4 0.0 reduce-scatter.2.cloned.1.call-update
  427.5 554.4 %reduce-scatter.2.cloned.1.call-done = f32[1024,2048]{1,0:T(8,128)} async-done(((f32[4096,2048]{1,0:T(8,128)}), f32[1024,2048]{1,0:T(8,128)}) %reduce-scatter.2.cloned.1.call-update) | async-done | bytes 8388624 | tf_op jit(solution)/shard_map/reduce_scatter | solution.py:27
  (1 shorter events, 0.0 us)
Async XLA Ops:
  6.5 340.8 %all-gather.2.cloned.1.call-start = ((), (), s32[]{:S(2)}) async-start(), calls=%async_computation.1 | async-start | bytes 25165824 | tf_op jit(solution)/shard_map/all_gather | solution.py:24
  6.5 93.9 %collective-permute-start = (bf16[4096,1024]{1,0:T(8,128)(2,1)}, bf16[4096,1024]{1,0:T(8,128)(2,1)}, u32[]{:S(2)}, u32[]{:S(2)}) collective-permute-start(bf16[4096,1024]{1,0:T(8,128)(2,1)} %param.3), channel_id=1, source_target_pairs={{0,1},{1,2},{2,3},{3,0},{4,5},{5,6},{6,7},{7,4},{8,9},{9,10},{10,1... | collective-permute-start | bytes 25165832 | tf_op jit(solution)/shard_map/ppermute | solution.py:20
  100.4 93.2 %collective-permute-start.1 = (bf16[4096,1024]{1,0:T(8,128)(2,1)}, bf16[4096,1024]{1,0:T(8,128)(2,1)}, u32[]{:S(2)}, u32[]{:S(2)}) collective-permute-start(bf16[4096,1024]{1,0:T(8,128)(2,1)} %collective-permute-done), channel_id=1, source_target_pairs={{0,1},{1,2},{2,3},{3,0},{4,5},{5,6},{6,7},{7,4},{8,9},{9,10},{10,1... | collective-permute-start | bytes 25165832 | tf_op jit(solution)/shard_map/ppermute | solution.py:20
  100.4 881.4 %reduce-scatter.2.cloned.1.call-start = ((), (), s32[]{:S(2)}) async-start(), calls=%async_computation.2 | async-start | bytes 41943040 | tf_op jit(solution)/shard_map/reduce_scatter | solution.py:27
  193.6 93.2 %collective-permute-start.2 = (bf16[4096,1024]{1,0:T(8,128)(2,1)}, bf16[4096,1024]{1,0:T(8,128)(2,1)}, u32[]{:S(2)}, u32[]{:S(2)}) collective-permute-start(bf16[4096,1024]{1,0:T(8,128)(2,1)} %collective-permute-done.1), channel_id=1, source_target_pairs={{0,1},{1,2},{2,3},{3,0},{4,5},{5,6},{6,7},{7,4},{8,9},{9,10},{10,1... | collective-permute-start | bytes 25165832 | tf_op jit(solution)/shard_map/ppermute | solution.py:20
Sparse Core Ops, SparseCore 0:
  100.6 201.1 all-gather.1
  427.6 554.2 reduce-scatter.1
